TPU v7x, 32 devices: a whole 2x2x4 slice. The times are simulated.
32 devices in a mesh: rep: 16 (over z, y, core), grp: 2 (over x).
Axes of the slice: x: 2, y: 2, z: 4, core: 2. Of those that a mesh axis runs over, the one named last changes fastest.
Arguments:
- local_params: bfloat16 [16, 2, 32, 8192], P('rep', 'grp'), may hold values from -130 to 130
- snapshot: bfloat16 [2, 32, 8192], P('grp'), may hold values from -4 to 4
- master: float32 [2, 32, 8192], P('grp', 'rep'), may hold values from -6 to 6
- momentum: float32 [2, 32, 8192], P('grp', 'rep'), may hold values from -4 to 4
Outputs:
- new_master: float32 [2, 32, 8192], P('grp', 'rep')
- new_momentum: float32 [2, 32, 8192], P('grp', 'rep')
- new_params: bfloat16 [2, 32, 8192], P('grp')
All inputs are finite; a program needn't handle non-finite values.
Results may differ from a plain program's by a relative error of at most 0.001.
Values may be sent and summed in bfloat16 or wider, within the bound.
A program may use at most 128 MiB of HBM per device.

v0:
```python
import jax
import jax.numpy as jnp
from jax import lax
from jax.sharding import PartitionSpec as P

nesterov_mu = 0.9
outer_rate = 0.7
clip_limit = 0.15
epsilon = 1e-06


def body(local_params, snapshot, master, momentum):
    replicas = lax.axis_size("rep")
    own_rows = master.shape[1]
    replica_sum = jnp.sum(
        lax.all_to_all(local_params[0], "rep", split_axis=1, concat_axis=0, tiled=True).astype(
            jnp.float32
        ),
        axis=0,
        keepdims=True,
    )
    owned_snap = lax.dynamic_slice_in_dim(
        snapshot, lax.axis_index("rep") * own_rows, own_rows, 1
    ).astype(jnp.float32)
    outer_grad = owned_snap - replica_sum / replicas
    elements = snapshot.shape[1] * snapshot.shape[2] * lax.axis_size("grp")
    squares = lax.psum(jnp.sum(outer_grad * outer_grad), ("rep", "grp"))
    grad_rms = jnp.sqrt(squares / elements + epsilon)
    clipped = jnp.minimum(1.0, clip_limit / grad_rms) * outer_grad
    new_momentum = nesterov_mu * momentum + clipped
    new_master = master - outer_rate * (clipped + nesterov_mu * new_momentum)
    new_params = lax.all_gather(new_master.astype(jnp.bfloat16), "rep", axis=1, tiled=True)
    return (new_master, new_momentum, new_params)


def solution(mesh):
    return jax.shard_map(
        body,
        mesh=mesh,
        in_specs=(
            P("rep", "grp", None, None),
            P("grp", None, None),
            P("grp", "rep", None),
            P("grp", "rep", None),
        ),
        out_specs=(P("grp", "rep", None), P("grp", "rep", None), P("grp", None, None)),
        check_vma=False,
    )
```

profile of v0, /device:TPU:0, one launch (start us, length us, event | category | flops | bytes accessed | tf_op | source)
XLA Modules:
  0.0 102.9 jit_solution(10499969501519827075)
XLA Ops:
  0.6 0.0 copy-start
  0.6 2.2 %copy.40 = bf16[1,32,8192]{2,0,1:T(2,128)(2,1)S(1)} copy(bf16[1,32,8192]{2,1,0:T(8,128)(2,1)} %bitcast.7) | data formatting | bytes 1048576 | tf_op jit(solution)/shard_map/squeeze | solution.py:16
  2.9 0.5 broadcast.18
  3.4 3.8 %reduce.2 = bf16[32,8192]{1,0:T(8,128)(2,1)S(1)} reduce(bf16[32,1,8192]{2,1,0:T(2,128)(2,1)S(1)} %bitcast.6, bf16[]{:T(256)} %broadcast.18), dimensions={1}, to_apply=%bitcast.5.reduce_sub_computation | reduce | bytes 1048578
  7.2 1.1 %reshape.23 = bf16[16,2,8192]{2,1,0:T(2,128)(2,1)} reshape(bf16[32,8192]{1,0:T(8,128)(2,1)S(1)} %reduce.2) | data formatting | bytes 1048576
  8.3 7.4 %all-to-all-start = ((bf16[16,2,8192]{2,1,0:T(2,128)(2,1)}), bf16[16,2,8192]{2,1,0:T(2,128)(2,1)S(1)}, u32[]{:S(2)}, u32[]{:S(2)}) async-start(bf16[16,2,8192]{2,1,0:T(2,128)(2,1)} %reshape.23), calls=%async_computation | async-start | bytes 1048576 | tf_op jit(solution)/shard_map/all_to_all | solution.py:16
  15.7 0.0 copy-done
  15.8 14.2 %all-to-all-done = bf16[16,2,8192]{2,1,0:T(2,128)(2,1)S(1)} async-done(((bf16[16,2,8192]{2,1,0:T(2,128)(2,1)}), bf16[16,2,8192]{2,1,0:T(2,128)(2,1)S(1)}, u32[]{:S(2)}, u32[]{:S(2)}) %all-to-all-start) | async-done | bytes 524320 | tf_op jit(solution)/shard_map/all_to_all | solution.py:16
  30.0 0.5 reshape.24
  30.5 3.0 %convert_reduce_fusion = f32[32,8192]{1,0:T(8,128)S(1)} fusion(bf16[32,1,8192]{2,1,0:T(2,128)(2,1)S(1)} %reshape.24), kind=kLoop, calls=%fused_computation | loop fusion | flops 262144 | bytes 1572864 | tf_op jit(solution)/shard_map/convert_element_type | solution.py:16
  33.6 0.6 reshape.21
  34.2 0.4 reduce_sum.18
  34.6 0.0 copy-start.1
  34.6 0.7 multiply_reduce_fusion
  35.4 0.1 copy-done.1
  35.5 0.0 copy-start.2
  35.5 39.8 %psum.7 = f32[]{:T(128)} all-reduce(f32[]{:T(128)} %multiply_reduce_fusion), channel_id=1, replica_groups=mesh['rep'=16,'grp'=2] {'rep','grp'}, use_global_device_ids=true, to_apply=%region_2.0 | all-reduce | flops 1 | bytes 8 | tf_op jit(solution)/shard_map/psum | solution.py:27
  76.0 0.0 copy-done.2
  76.0 0.2 fusion.1
  76.3 0.7 copy.19
  76.9 0.7 copy.20
  77.6 23.9 %all_gather.3 = bf16[1,32,8192]{2,0,1:T(2,128)(2,1)S(1)} all-gather(bf16[1,2,8192]{2,0,1:T(2,128)(2,1)S(1)} %get-tuple-element.9), channel_id=1, replica_groups=mesh['rep'=16,'grp'=2] {'rep'}, dimensions={1}, use_global_device_ids=true | all-gather | bytes 557056 | tf_op jit(solution)/shard_map/all_gather | solution.py:32
  101.5 1.4 %copy.21 = bf16[1,32,8192]{2,1,0:T(8,128)(2,1)} copy(bf16[1,32,8192]{2,0,1:T(2,128)(2,1)S(1)} %all_gather.3) | data formatting | bytes 1048576
  (3 shorter events, 0.1 us)
Async XLA Ops:
  0.6 15.1 %copy-start = (bf16[1,32,8192]{2,1,0:T(8,128)(2,1)S(1)}, bf16[1,32,8192]{2,1,0:T(8,128)(2,1)}, u32[]{:S(2)}) copy-start(bf16[1,32,8192]{2,1,0:T(8,128)(2,1)} %param.5) | copy-start | bytes 1572868
  8.3 21.7 %all-to-all-start = ((bf16[16,2,8192]{2,1,0:T(2,128)(2,1)}), bf16[16,2,8192]{2,1,0:T(2,128)(2,1)S(1)}, u32[]{:S(2)}, u32[]{:S(2)}) async-start(bf16[16,2,8192]{2,1,0:T(2,128)(2,1)} %reshape.23), calls=%async_computation | async-start | bytes 1048576 | tf_op jit(solution)/shard_map/all_to_all | solution.py:16
  34.6 0.8 copy-start.1
  35.5 40.5 %copy-start.2 = (f32[1,2,8192]{2,1,0:T(2,128)S(1)}, f32[1,2,8192]{2,1,0:T(2,128)}, u32[]{:S(2)}) copy-start(f32[1,2,8192]{2,1,0:T(2,128)} %param.6) | copy-start | bytes 196612
where the time goes:
time: 103 us
  blocking collectives  63.7 us (62%)
  waiting for transfers between devices  14.2 us (14%)
  other arithmetic  8.25 us (8%)
  local copies, waits for them, and re-layouts  7.88 us (8%)
  starting transfers between devices  7.41 us (7%)
  between operations  1.45 us (1%)
    psum x1, blocking collectives, body(): squares = lax.psum(jnp.sum(outer_grad * outer_grad), ('rep', 'grp'))  39.8 us
    all_gather x1, blocking collectives, body(): lax.all_gather(new_master.astype(jnp.bfloat16), 'rep', axis=1, tiled=True)  23.9 us
    all_to_all x1, waiting for transfers between devices, body(): lax.all_to_all(local_params[0], 'rep', split_axis=1, concat_axis=0, tiled...  14.2 us
    all_to_all x1, starting transfers between devices, body(): lax.all_to_all(local_params[0], 'rep', split_axis=1, concat_axis=0, tiled...  7.41 us
    unnamed x12, local copies, waits for them, and re-layouts  5.01 us
    unnamed x1, other arithmetic  3.81 us
    convert_element_type x1, other arithmetic, body(): lax.all_to_all(local_params[0], 'rep', split_axis=1, concat_axis=0, tiled...  3.02 us
    squeeze x1, local copies, waits for them, and re-layouts, body(): local_params[0]  2.2 us
  transfers between devices with their start and end apart: 1, of which 1 were waited for; matrix products, arithmetic and copies ran while one was open for 0% of the time, Pallas kernels for 0%

commit v1 on v0

--- a/solution.py
+++ b/solution.py
@@ -13,9 +13,12 @@
     replicas = lax.axis_size("rep")
     own_rows = master.shape[1]
     replica_sum = jnp.sum(
-        lax.all_to_all(local_params[0], "rep", split_axis=1, concat_axis=0, tiled=True).astype(
-            jnp.float32
-        ),
+        jnp.concatenate(
+            lax.all_to_all(
+                jnp.stack(jnp.split(local_params[0], lax.axis_size("rep"), axis=1)), "rep", 0, 0
+            ),
+            axis=0,
+        ).astype(jnp.float32),
         axis=0,
         keepdims=True,
     )

time: 103 us -> 109 us (1.058)
  local copies, waits for them, and re-layouts: 7.88 us -> 20.5 us
  other arithmetic: 8.25 us -> 1.47 us
    unnamed x12 -> x26, local copies, waits for them, and re-layouts: 5.01 us -> 19.9 us
    unnamed x1 -> x0, other arithmetic: 3.81 us -> none
    convert_element_type x1 -> x0, other arithmetic: 3.02 us -> none  [body(): lax.all_to_all(local_params[0], 'rep', split_axis=1, concat_axis=0, tiled...]
    squeeze x1 -> x0, local copies, waits for them, and re-layouts: 2.2 us -> none  [body(): local_params[0]]
where the time goes in v1:
time: 109 us
  blocking collectives  63.7 us (58%)
  local copies, waits for them, and re-layouts  20.5 us (19%)
  waiting for transfers between devices  14.2 us (13%)
  starting transfers between devices  7.41 us (7%)
  other arithmetic  1.47 us (1%)
  between operations  1.42 us (1%)
    psum x1, blocking collectives, body(): squares = lax.psum(jnp.sum(outer_grad * outer_grad), ('rep', 'grp'))  39.8 us
    all_gather x1, blocking collectives, body(): lax.all_gather(new_master.astype(jnp.bfloat16), 'rep', axis=1, tiled=True)  23.9 us
    unnamed x26, local copies, waits for them, and re-layouts  19.9 us
    all_to_all x1, waiting for transfers between devices, body(): lax.all_to_all(jnp.stack(jnp.split(local_params[0], lax.axis_size('rep'),...  14.2 us
    all_to_all x1, starting transfers between devices, body(): lax.all_to_all(jnp.stack(jnp.split(local_params[0], lax.axis_size('rep'),...  7.41 us
  transfers between devices with their start and end apart: 1, of which 1 were waited for; matrix products, arithmetic and copies ran while one was open for 0% of the time, Pallas kernels for 0%

profile of v1, /device:TPU:0, one launch (start us, length us, event | category | flops | bytes accessed | tf_op | source)
XLA Modules:
  0.0 108.8 jit_solution(14995001041123533205)
XLA Ops:
  0.6 0.0 copy-start
  0.6 0.0 copy-start.1
  0.7 1.6 %constant_dynamic-update-slice_fusion.15 = bf16[16,1,2,8192]{3,2,1,0:T(2,128)(2,1)} fusion(bf16[1,32,8192]{2,1,0:T(8,128)(2,1)} %bitcast.65), kind=kLoop, calls=%fused_computation.21 | loop fusion | bytes 65536
  2.3 1.6 %constant_dynamic-update-slice_fusion.14 = bf16[16,1,2,8192]{3,2,1,0:T(2,128)(2,1)} fusion(bf16[16,1,2,8192]{3,2,1,0:T(2,128)(2,1)} %constant_dynamic-update-slice_fusion.15, bf16[1,32,8192]{2,1,0:T(8,128)(2,1)} %bitcast.66), kind=kLoop, calls=%fused_computation.20 | loop fusion | bytes 65536
  3.8 1.6 %constant_dynamic-update-slice_fusion.13 = bf16[16,1,2,8192]{3,2,1,0:T(2,128)(2,1)} fusion(bf16[16,1,2,8192]{3,2,1,0:T(2,128)(2,1)} %constant_dynamic-update-slice_fusion.14, bf16[1,32,8192]{2,1,0:T(8,128)(2,1)} %bitcast.67), kind=kLoop, calls=%fused_computation.19 | loop fusion | bytes 65536
  5.4 1.6 %constant_dynamic-update-slice_fusion.12 = bf16[16,1,2,8192]{3,2,1,0:T(2,128)(2,1)} fusion(bf16[16,1,2,8192]{3,2,1,0:T(2,128)(2,1)} %constant_dynamic-update-slice_fusion.13, bf16[1,32,8192]{2,1,0:T(8,128)(2,1)} %bitcast.68), kind=kLoop, calls=%fused_computation.18 | loop fusion | bytes 65536
  6.9 1.5 %constant_dynamic-update-slice_fusion.11 = bf16[16,1,2,8192]{3,2,1,0:T(2,128)(2,1)} fusion(bf16[16,1,2,8192]{3,2,1,0:T(2,128)(2,1)} %constant_dynamic-update-slice_fusion.12, bf16[1,32,8192]{2,1,0:T(8,128)(2,1)} %bitcast.69), kind=kLoop, calls=%fused_computation.17 | loop fusion | bytes 65536
  8.5 1.6 %constant_dynamic-update-slice_fusion.10 = bf16[16,1,2,8192]{3,2,1,0:T(2,128)(2,1)} fusion(bf16[16,1,2,8192]{3,2,1,0:T(2,128)(2,1)} %constant_dynamic-update-slice_fusion.11, bf16[1,32,8192]{2,1,0:T(8,128)(2,1)} %bitcast.70), kind=kLoop, calls=%fused_computation.16 | loop fusion | bytes 65536
  10.0 1.6 %constant_dynamic-update-slice_fusion.9 = bf16[16,1,2,8192]{3,2,1,0:T(2,128)(2,1)} fusion(bf16[16,1,2,8192]{3,2,1,0:T(2,128)(2,1)} %constant_dynamic-update-slice_fusion.10, bf16[1,32,8192]{2,1,0:T(8,128)(2,1)} %bitcast.71), kind=kLoop, calls=%fused_computation.15 | loop fusion | bytes 65536
  11.6 1.6 %constant_dynamic-update-slice_fusion.8 = bf16[16,1,2,8192]{3,2,1,0:T(2,128)(2,1)} fusion(bf16[16,1,2,8192]{3,2,1,0:T(2,128)(2,1)} %constant_dynamic-update-slice_fusion.9, bf16[1,32,8192]{2,1,0:T(8,128)(2,1)} %bitcast.72), kind=kLoop, calls=%fused_computation.14 | loop fusion | bytes 65536
  13.1 0.0 copy-done.1
  13.1 0.6 constant_dynamic-update-slice_fusion.7
  13.8 0.7 constant_dynamic-update-slice_fusion.6
  14.4 0.7 constant_dynamic-update-slice_fusion.5
  15.1 0.7 constant_dynamic-update-slice_fusion.4
  15.7 0.6 constant_dynamic-update-slice_fusion.3
  16.4 0.7 constant_dynamic-update-slice_fusion.2
  17.0 0.7 constant_dynamic-update-slice_fusion.1
  17.7 0.7 constant_dynamic-update-slice_fusion
  18.3 7.4 %all-to-all-start = ((bf16[16,1,2,8192]{3,2,1,0:T(2,128)(2,1)}), bf16[16,1,2,8192]{3,2,1,0:T(2,128)(2,1)S(1)}, u32[]{:S(2)}, u32[]{:S(2)}) async-start(bf16[16,1,2,8192]{3,2,1,0:T(2,128)(2,1)} %constant_dynamic-update-slice_fusion), calls=%async_computation | async-start | bytes 1048576 | tf_op jit(solution)/shard_map/all_to_all | solution.py:17
  25.7 0.0 copy-done
  25.8 14.2 %all-to-all-done = bf16[16,1,2,8192]{3,2,1,0:T(2,128)(2,1)S(1)} async-done(((bf16[16,1,2,8192]{3,2,1,0:T(2,128)(2,1)}), bf16[16,1,2,8192]{3,2,1,0:T(2,128)(2,1)S(1)}, u32[]{:S(2)}, u32[]{:S(2)}) %all-to-all-start) | async-done | bytes 524320 | tf_op jit(solution)/shard_map/all_to_all | solution.py:17
  40.0 0.4 convert_reduce_fusion
  40.5 0.0 copy-start.2
  40.5 0.7 multiply_reduce_fusion
  41.2 0.1 copy-done.2
  41.3 0.0 copy-start.3
  41.4 39.8 %psum.7 = f32[]{:T(128)} all-reduce(f32[]{:T(128)} %multiply_reduce_fusion), channel_id=1, replica_groups=mesh['rep'=16,'grp'=2] {'rep','grp'}, use_global_device_ids=true, to_apply=%region_2.0 | all-reduce | flops 1 | bytes 8 | tf_op jit(solution)/shard_map/psum | solution.py:30
  81.9 0.0 copy-done.3
  81.9 0.2 fusion.1
  82.1 0.7 copy.11
  82.8 0.7 copy.12
  83.5 23.9 %all_gather.3 = bf16[1,32,8192]{2,0,1:T(2,128)(2,1)S(1)} all-gather(bf16[1,2,8192]{2,0,1:T(2,128)(2,1)S(1)} %get-tuple-element.6), channel_id=1, replica_groups=mesh['rep'=16,'grp'=2] {'rep'}, dimensions={1}, use_global_device_ids=true | all-gather | bytes 557056 | tf_op jit(solution)/shard_map/all_gather | solution.py:35
  107.4 1.4 %copy.13 = bf16[1,32,8192]{2,1,0:T(8,128)(2,1)} copy(bf16[1,32,8192]{2,0,1:T(2,128)(2,1)S(1)} %all_gather.3) | data formatting | bytes 1048576
  (3 shorter events, 0.1 us)
Async XLA Ops:
  0.6 25.1 %copy-start = (bf16[1,32,8192]{2,1,0:T(8,128)(2,1)S(1)}, bf16[1,32,8192]{2,1,0:T(8,128)(2,1)}, u32[]{:S(2)}) copy-start(bf16[1,32,8192]{2,1,0:T(8,128)(2,1)} %param.5) | copy-start | bytes 1572868
  0.6 12.5 %copy-start.1 = (bf16[1,1,32,8192]{3,2,1,0:T(8,128)(2,1)S(1)}, bf16[1,1,32,8192]{3,2,1,0:T(8,128)(2,1)}, u32[]{:S(2)}) copy-start(bf16[1,1,32,8192]{3,2,1,0:T(8,128)(2,1)} %param.4) | copy-start | bytes 1572868
  18.3 21.7 %all-to-all-start = ((bf16[16,1,2,8192]{3,2,1,0:T(2,128)(2,1)}), bf16[16,1,2,8192]{3,2,1,0:T(2,128)(2,1)S(1)}, u32[]{:S(2)}, u32[]{:S(2)}) async-start(bf16[16,1,2,8192]{3,2,1,0:T(2,128)(2,1)} %constant_dynamic-update-slice_fusion), calls=%async_computation | async-start | bytes 1048576 | tf_op jit(solution)/shard_map/all_to_all | solution.py:17
  40.5 0.8 copy-start.2
  41.3 40.5 %copy-start.3 = (f32[1,2,8192]{2,1,0:T(2,128)S(1)}, f32[1,2,8192]{2,1,0:T(2,128)}, u32[]{:S(2)}) copy-start(f32[1,2,8192]{2,1,0:T(2,128)} %param.6) | copy-start | bytes 196612
